TPU v7x, 32 devices: a whole 2x2x4 slice. The times are simulated.
32 devices in a mesh: tm: 8 (over z, x), env: 4 (over y, core).
Axes of the slice: x: 2, y: 2, z: 4, core: 2. Of those that a mesh axis runs over, the one named last changes fastest.
Arguments:
- features: bfloat16 [512, 64, 4096], P('tm', 'env'), may hold values from -6 to 6
- w_hidden: bfloat16 [4096, 1024], P('tm'), may hold values from -0.09375 to 0.09375
- b_hidden: float32 [1024], replicated, may hold values from -3 to 3
- w_value: float32 [1024], replicated, may hold values from -0.1875 to 0.1875
- w_policy: bfloat16 [4096, 256], P('tm'), may hold values from -15.0625 to 15.0625
- old_value: float32 [512, 64], P('tm', 'env'), may hold values from -6 to 6
- rewards: float32 [512, 64], P('tm', 'env'), may hold values from -0.3 to 0.3
- dones: int32 [512, 64], P('tm', 'env'), may hold values 0 or 1
- discounts: float32 [2, 64], P(None, 'env'), may hold values from 0.98333333 to 1, as said below
- last_value: float32 [64], P('env'), may hold values from -6 to 6
- actions: int32 [512, 64], P('tm', 'env'), may hold values from 0 to 255
- old_logprob: float32 [512, 64], P('tm', 'env'), may hold values from -7 to -4.5
Outputs:
- norm_adv: float32 [512, 64], P('tm', 'env')
- value_pred: float32 [512, 64], P('tm', 'env')
- new_logprob: float32 [512, 64], P('tm', 'env')
- losses: float32 [2], replicated
Inputs may be any that keep to these rules, and one draw needn't show every extreme that they name: `discounts`: every entry is below 1.
All inputs are finite; a program needn't handle non-finite values. No bound on the sum of `dones` on one device may be relied on, other than what follows from the above.
Results may differ from a plain program's by a relative error of at most 0.0003.
Values may be sent and summed in bfloat16 or wider, within the bound.
A program may use at most 64 MiB of HBM per device.

v0:
```python
import jax
import jax.numpy as jnp
from jax import lax
from jax.sharding import PartitionSpec as P


def passed_along(block, axis, distance):
    devices = range(lax.axis_size(axis))
    route = [(i - distance, i) for i in devices if i - distance in devices]
    return lax.ppermute(block, axis, route)


def carried_in(array, axis, combine, identity):
    length, here = (lax.axis_size(axis), lax.axis_index(axis))
    everything = jax.tree.map(lambda part: lax.all_gather(part, axis), array)
    start = jax.tree.map(
        lambda part, zero: jnp.broadcast_to(jnp.asarray(zero, part.dtype), part.shape),
        array,
        identity,
    )

    def turn(k, before):
        at = length - 1 - k
        reached = at > here
        new = combine(before, jax.tree.map(lambda part: part[at], everything))
        return jax.tree.map(lambda a, b: jnp.where(reached, a, b), new, before)

    return lax.fori_loop(0, length, turn, start)


def block_terms(step_rewards, step_values, step_keep, gamma, lam, value_after):
    steps = step_rewards.shape[0]
    decay = gamma * lam
    rowpos = lax.broadcasted_iota(jnp.int32, (steps, steps), 0)
    colpos = lax.broadcasted_iota(jnp.int32, (steps, steps), 1)
    lower = (colpos < rowpos).astype(jnp.float32)
    ended = jnp.dot(lower, 1.0 - step_keep, precision=lax.Precision.HIGHEST)
    lag = (colpos - rowpos).astype(jnp.float32)
    unbroken = ended[None, :, :] == ended[:, None, :]
    power = jnp.exp(lag[:, :, None] * jnp.log(decay)[None, None, :])
    matrix = jnp.where((colpos >= rowpos)[:, :, None] & unbroken, power, 0.0)
    shifted = jnp.concatenate([step_values[1:], value_after[None]], 0)
    delta = step_rewards + gamma * step_keep * shifted - step_values
    local = jnp.einsum("tse,se->te", matrix, delta, precision=lax.Precision.HIGHEST)
    gain = matrix[:, -1, :] * (decay * step_keep[-1])[None, :]
    tail = matrix[:, -1, :] * (gamma * step_keep[-1])[None, :]
    return (local, gain, tail)


def chain(earlier, later):
    return (later[0] * earlier[0], later[1] + later[0] * earlier[1])


def shards(
    features,
    w_hidden,
    b_hidden,
    w_value,
    w_policy,
    old_value,
    rewards,
    dones,
    discounts,
    last_value,
    actions,
    old_logprob,
):
    tsteps, envs, width = features.shape
    rows = features.reshape(tsteps * envs, width)
    portion = w_hidden.shape[0] // lax.axis_size("env")
    offset = lax.axis_index("env") * portion
    hidden_part = lax.dynamic_slice_in_dim(w_hidden, offset, portion, 0)
    policy_part = lax.dynamic_slice_in_dim(w_policy, offset, portion, 0)
    hidden_w, policy_w = (
        lax.all_gather(hidden_part, ("tm", "env"), axis=0, tiled=True),
        lax.all_gather(policy_part, ("tm", "env"), axis=0, tiled=True),
    )
    pre = jnp.dot(rows, hidden_w, preferred_element_type=jnp.float32) + b_hidden
    hidden_act = jnp.tanh(pre)
    value_pred = jnp.dot(hidden_act, w_value, precision=lax.Precision.HIGHEST).reshape(tsteps, envs)
    logits = jnp.dot(rows, policy_w, preferred_element_type=jnp.float32)
    logp = jax.nn.log_softmax(logits, axis=-1)
    choose = lax.broadcasted_iota(jnp.int32, logp.shape, 1) == actions.reshape(-1)[:, None]
    new_logprob = jnp.sum(jnp.where(choose, logp, 0.0), axis=1).reshape(tsteps, envs)
    keep = 1.0 - dones.astype(jnp.float32)
    gamma = discounts[0]
    lam = discounts[1]
    position = lax.axis_index("tm")
    final = lax.axis_size("tm") - 1
    ones = jnp.ones((envs,), jnp.float32)
    zeros = jnp.zeros((envs,), jnp.float32)
    following = passed_along(old_value[0], "tm", -1)
    value_after = jnp.where(position == final, last_value, following)
    local, gain, tail = block_terms(rewards, old_value, keep, gamma, lam, value_after)
    carried = carried_in((gain[0], local[0]), "tm", chain, (ones, zeros))
    advantage = local + gain * carried[1][None, :]
    count = tsteps * envs * lax.axis_size("tm") * lax.axis_size("env")
    total, square = lax.psum((jnp.sum(advantage), jnp.sum(advantage * advantage)), ("tm", "env"))
    adv_mean = total / count
    adv_var = square / count - adv_mean * adv_mean
    norm_adv = (advantage - adv_mean) / jnp.sqrt(adv_var + 0.25)
    ratio = jnp.exp(new_logprob - old_logprob)
    policy_term = -jnp.minimum(ratio * norm_adv, jnp.clip(ratio, 0.8, 1.2) * norm_adv)
    returns = advantage + old_value
    clipped = old_value + jnp.clip(value_pred - old_value, -0.2, 0.2)
    value_term = 0.5 * jnp.maximum((value_pred - returns) ** 2, (clipped - returns) ** 2)
    policy_sum, value_sum = lax.psum((jnp.sum(policy_term), jnp.sum(value_term)), ("tm", "env"))
    losses = jnp.stack([policy_sum, value_sum]) / count
    return (norm_adv, value_pred, new_logprob, losses)


def solution(mesh):
    in_specs = (
        P("tm", "env", None),
        P("tm", None),
        P(),
        P(),
        P("tm", None),
        P("tm", "env"),
        P("tm", "env"),
        P("tm", "env"),
        P(None, "env"),
        P("env"),
        P("tm", "env"),
        P("tm", "env"),
    )
    out_specs = (P("tm", "env"), P("tm", "env"), P("tm", "env"), P())
    return jax.shard_map(shards, mesh=mesh, in_specs=in_specs, out_specs=out_specs, check_vma=False)
```

profile of v0, /device:TPU:0, one launch (start us, length us, event | category | flops | bytes accessed | tf_op | source)
XLA Modules:
  0.0 258.0 jit_solution(8669680264594907318)
XLA Ops:
  7.2 0.0 copy-start
  7.2 0.0 all-gather.7.cloned.1.call-start
  7.2 1.5 constant_dynamic-slice_fusion
  8.8 0.0 all-gather.7.cloned.1.call-update
  8.8 0.0 all-gather.5.cloned.1.call-start
  8.8 0.0 copy-done
  8.9 0.7 constant_dynamic-slice_fusion.1
  9.6 0.0 all-gather.5.cloned.1.call-update
  9.6 0.8 slice_reduce_fusion.2
  10.4 1.3 collective-permute-start
  11.7 0.8 slice.25
  12.5 0.8 copy.65
  13.3 0.1 eq.30
  13.4 0.8 fusion.9
  14.2 0.1 copy.63
  14.3 0.8 fusion.19
  15.1 0.1 copy.74
  15.1 0.1 copy.75
  15.3 0.8 fusion.17
  16.0 0.2 exponential_select_fusion
  16.3 0.6 collective-permute-done
  16.9 0.1 copy.62
  16.9 0.8 convert_subtract_fusion
  17.7 0.7 fusion.7
  18.4 0.1 slice_reduce_fusion.1
  18.5 23.5 %all-gather = f32[8,1,16]{2,1,0:T(1,128)S(1)} all-gather(f32[1,1,16]{2,1,0:T(1,128)S(1)} %bitcast.64), channel_id=1, replica_groups=mesh['tm'=8,'env'=4] {'tm'}, dimensions={0}, use_global_device_ids=true | all-gather | bytes 576 | tf_op jit(solution)/shard_map/all_gather | solution.py:15
  42.0 0.2 fusion.10
  42.2 0.1 fusion.11
  42.3 0.1 slice_reduce_fusion
  42.4 16.3 %all-gather.1 = f32[8,1,16]{2,1,0:T(1,128)S(1)} all-gather(f32[1,1,16]{2,1,0:T(1,128)S(1)} %bitcast.63), channel_id=1, replica_groups=mesh['tm'=8,'env'=4] {'tm'}, dimensions={0}, use_global_device_ids=true | all-gather | bytes 576 | tf_op jit(solution)/shard_map/all_gather | solution.py:15
  58.7 0.4 while.16
  59.0 10.8 %all-gather.7.cloned.1.call-done = bf16[4096,256]{1,0:T(8,128)(2,1)} async-done(((bf16[128,256]{1,0:T(8,128)(2,1)}), bf16[4096,256]{1,0:T(8,128)(2,1)}) %all-gather.7.cloned.1.call-update) | async-done | bytes 2097168 | tf_op jit(solution)/shard_map/all_gather | solution.py:76
  69.8 6.4 %fusion.20 = (f32[1024]{0:T(1024)S(1)}, f32[256,1024]{1,0:T(8,128)S(1)}) fusion(bf16[4096,256]{1,0:T(8,128)(2,1)} %all-gather.7.cloned.1.call-done, bf16[1024,4096]{1,0:T(8,128)(2,1)} %bitcast.65), kind=kOutput, calls=%fused_computation.48 | convolution fusion | flops 2147744768 | bytes 11538432 | tf_op jit(solution)/shard_map/dot_general | solution.py:81
  76.2 0.2 exponential_reduce_fusion
  76.4 0.2 fusion.6
  76.6 0.1 reshape.54
  76.7 0.1 copy.70
  76.8 0.0 copy-start.2
  76.8 0.0 copy-start.5
  76.8 0.0 copy-start.6
  76.8 71.9 %all-gather.5.cloned.1.call-done = bf16[4096,1024]{1,0:T(8,128)(2,1)} async-done(((bf16[128,1024]{1,0:T(8,128)(2,1)}), bf16[4096,1024]{1,0:T(8,128)(2,1)}) %all-gather.5.cloned.1.call-update) | async-done | bytes 8388624 | tf_op jit(solution)/shard_map/all_gather | solution.py:75
  148.6 12.7 %fusion.21 = f32[1024,1024]{1,0:T(8,128)S(1)} fusion(bf16[4096,1024]{1,0:T(8,128)(2,1)} %all-gather.5.cloned.1.call-done, bf16[1024,4096]{1,0:T(8,128)(2,1)} %bitcast.66), kind=kOutput, calls=%fused_computation.49 | convolution fusion | flops 8589934592 | bytes 20971520 | tf_op jit(solution)/shard_map/dot_general | solution.py:78
  161.4 0.0 copy-start.1
  161.4 0.0 copy-start.4
  161.4 0.0 copy-done.5
  161.4 0.0 copy-done.6
  161.4 2.6 %fusion.1 = f32[1,1024]{1,0:T(1,128)S(1)} fusion(f32[1024,1]{0,1:T(1,128)S(1)} %bitcast.62, f32[1024,1024]{1,0:T(8,128)S(1)} %fusion.21, f32[1024]{0:T(1024)S(1)} %copy-done.6), kind=kOutput, calls=%fused_computation.4 | convolution fusion | flops 13631488 | bytes 4206592 | tf_op jit(solution)/shard_map/dot_general | solution.py:80
  164.0 0.1 reshape.53
  164.1 0.1 copy.69
  164.2 0.0 copy-start.3
  164.2 0.0 copy-done.1
  164.2 0.8 multiply_reduce_fusion
  164.9 39.4 %all-reduce.1 = (f32[]{:T(128)}, f32[]{:T(128)}) all-reduce(f32[]{:T(128)} %get-tuple-element.172, f32[]{:T(128)} %get-tuple-element.173), channel_id=1, replica_groups=mesh['tm'=8,'env'=4] {'tm','env'}, use_global_device_ids=true, to_apply=%region_5.6 | all-reduce | flops 2 | bytes 16 | tf_op jit(solution)/shard_map/psum | solution.py:98
  206.8 0.0 copy-done.2
  206.8 0.0 copy-done.4
  206.8 1.2 minimum_reduce_fusion
  208.6 40.9 %all-reduce = (f32[1]{0:T(128)}, f32[1]{0:T(128)}) all-reduce(f32[1]{0:T(128)} %bitcast.16, f32[1]{0:T(128)} %bitcast.15), channel_id=1, replica_groups=mesh['tm'=8,'env'=4] {'tm','env'}, use_global_device_ids=true, to_apply=%region_12.13 | all-reduce | flops 2 | bytes 16 | tf_op jit(solution)/shard_map/psum | solution.py:107
  249.4 1.8 maximum_multiply_fusion.1
  251.2 0.0 copy-done.3
  (13 shorter events, 0.2 us)
Async XLA Ops:
  7.2 1.7 copy-start
  7.2 62.6 %all-gather.7.cloned.1.call-start = ((), (), s32[]{:S(2)}) async-start(), calls=%async_computation.1 | async-start | bytes 2162688 | tf_op jit(solution)/shard_map/all_gather | solution.py:76
  8.8 139.8 %all-gather.5.cloned.1.call-start = ((), (), s32[]{:S(2)}) async-start(), calls=%async_computation | async-start | bytes 8650752 | tf_op jit(solution)/shard_map/all_gather | solution.py:75
  10.4 6.4 %collective-permute-start = (f32[16]{0:T(128)S(1)}, f32[16]{0:T(128)S(1)}, u32[]{:S(2)}, u32[]{:S(2)}) collective-permute-start(f32[16]{0:T(128)S(1)} %slice_reduce_fusion.2), channel_id=1, source_target_pairs={{4,0},{8,4},{12,8},{16,12},{20,16},{24,20},{28,24},{5,1},{9,5},{13... | collective-permute-start | bytes 200 | tf_op jit(solution)/shard_map/ppermute | solution.py:10
  76.8 130.0 %copy-start.2 = (f32[64,16]{0,1:T(8,128)}, f32[64,16]{0,1:T(8,128)S(1)}, u32[]{:S(2)}) copy-start(f32[64,16]{0,1:T(8,128)S(1)} %copy.70) | copy-start | bytes 12292
  76.8 84.6 %copy-start.5 = (f32[1024]{0:T(1024)S(1)}, f32[1024]{0:T(1024)}, u32[]{:S(2)}) copy-start(f32[1024]{0:T(1024)} %param.17) | copy-start | bytes 12292
  76.8 84.6 %copy-start.6 = (f32[1024]{0:T(1024)S(1)}, f32[1024]{0:T(1024)}, u32[]{:S(2)}) copy-start(f32[1024]{0:T(1024)} %param.16) | copy-start | bytes 12292
  161.4 2.8 %copy-start.1 = (f32[64,16]{0,1:T(8,128)S(1)}, f32[64,16]{0,1:T(8,128)}, u32[]{:S(2)}) copy-start(f32[64,16]{0,1:T(8,128)} %param.19) | copy-start | bytes 12292
  161.4 45.4 %copy-start.4 = (f32[64,16]{0,1:T(8,128)S(1)}, f32[64,16]{0,1:T(8,128)}, u32[]{:S(2)}) copy-start(f32[64,16]{0,1:T(8,128)} %param.25) | copy-start | bytes 12292
  164.2 87.1 %copy-start.3 = (f32[64,16]{0,1:T(8,128)}, f32[64,16]{0,1:T(8,128)S(1)}, u32[]{:S(2)}) copy-start(f32[64,16]{0,1:T(8,128)S(1)} %copy.69) | copy-start | bytes 12292
Sparse Core Ops, SparseCore 0:
  10.8 58.9 all-gather.6
  72.7 75.9 all-gather.4
where the time goes:
time: 259 us; the launch traced here: 258 us
  blocking collectives  120 us (46%)
  waiting for transfers between devices  83.3 us (32%)
  matrix products  23.2 us (9%)
  between operations  17.1 us (7%)
  local copies, waits for them, and re-layouts  6.42 us (2%)
  other arithmetic  6.37 us (2%)
    all_gather x1, waiting for transfers between devices, shards(): lax.all_gather(hidden_part, ('tm', 'env'), axis=0, tiled=True)  71.9 us
    psum x1, blocking collectives, shards(): lax.psum((jnp.sum(policy_term), jnp.sum(value_term)), ('tm', 'env'))  40.9 us
    all_gather x2, blocking collectives, carried_in(): everything = jax.tree.map(lambda part: lax.all_gather(part, axis), array)  39.8 us
    psum x1, blocking collectives, shards(): lax.psum((jnp.sum(advantage), jnp.sum(advantage * advantage)), ('tm', 'en...  39.4 us
    dot_general x1, matrix products, shards(): pre = jnp.dot(rows, hidden_w, preferred_element_type=jnp.float32) + b_hidden  12.7 us
    all_gather x1, waiting for transfers between devices, shards(): lax.all_gather(policy_part, ('tm', 'env'), axis=0, tiled=True)  10.8 us
    dot_general x1, matrix products, shards(): logits = jnp.dot(rows, policy_w, preferred_element_type=jnp.float32)  6.41 us
  transfers between devices with their start and end apart: 3, of which 3 were waited for; matrix products, arithmetic and copies ran while one was open for 6% of the time, Pallas kernels for 0%

commit v1 on v0

v1 whole, which is shorter than its diff:
```python
import functools

import jax
import jax.numpy as jnp
from jax import lax
from jax.experimental import pallas as pl
from jax.experimental.pallas import tpu as pltpu
from jax.sharding import PartitionSpec as P

MESH = pl.DeviceIdType.MESH
CORES = 2


def along_x(tm):
    nx = 1
    while (2 * nx) * (2 * nx) <= tm and tm % (2 * nx) == 0:
        nx *= 2
    return nx


def loop(count, body):
    if count == 1:
        body(0)
    elif count > 1:
        lax.fori_loop(0, count, lambda i, _: (body(i), 0)[1], 0)


def later(x, s, fill):
    return jnp.concatenate([x[s:], jnp.full((s, x.shape[1]), fill, x.dtype)], 0)


def kernel(
    sizes,
    feat_hbm,
    wh_hbm,
    wp_hbm,
    bias_ref,
    wv_ref,
    old_ref,
    rew_ref,
    done_ref,
    disc_ref,
    last_ref,
    act_ref,
    olp_ref,
    norm_ref,
    value_ref,
    logp_ref,
    loss_ref,
    feat,
    wa,
    wb,
    acca,
    accb,
    chain,
    stat,
    lsum,
    feat_sem,
    w_sem,
    recva,
    recvb,
    senda,
    sendb,
    chain_send,
    chain_recv,
    stat_send,
    stat_recv,
    lsum_send,
    lsum_recv,
):
    tmn, envn, steps, envs, shard, hid, acts = sizes
    nx = along_x(tmn)
    nz = tmn // nx
    ny = envn // CORES
    piece = shard // envn
    rows = steps * envs
    ca = wa.shape[1]
    ch = hid - ca
    n = tmn * envn
    ti = lax.axis_index("tm")
    ei = lax.axis_index("env")
    z, x = ti // nx, ti % nx
    y, c = ei // CORES, ei % CORES
    me = ti * envn + ei

    loads = [
        pltpu.make_async_copy(
            wh_hbm.at[:, pl.ds(0, ca)], wa.at[pl.ds(ti * shard, shard), :], w_sem.at[0]
        ),
        pltpu.make_async_copy(
            wh_hbm.at[:, pl.ds(ca, ch)],
            wb.at[pl.ds(ti * shard, shard), pl.ds(0, ch)],
            w_sem.at[1],
        ),
        pltpu.make_async_copy(
            wp_hbm, wb.at[pl.ds(ti * shard, shard), pl.ds(ch, acts)], w_sem.at[2]
        ),
    ]
    for load in loads:
        load.start()
    fetch = pltpu.make_async_copy(feat_hbm, feat, feat_sem)
    fetch.start()

    barrier = pltpu.get_barrier_semaphore()

    def greet(k):
        other = (me + 1 + k) % n
        pl.semaphore_signal(
            barrier,
            inc=1,
            device_id={"tm": other // envn, "env": other % envn},
            device_id_type=MESH,
        )

    loop(n - 1, greet)

    keep = 1.0 - done_ref[...].astype(jnp.float32)
    old = old_ref[...]
    gamma = disc_ref[0:1, :]
    lam = disc_ref[1:2, :]
    row = lax.broadcasted_iota(jnp.int32, (steps, envs), 0)
    gain = (gamma * lam) * keep
    base = rew_ref[...] + gamma * keep * later(old, 1, 0.0) - old
    tail = jnp.where(row == steps - 1, gamma * keep, 0.0)
    s = 1
    while s < steps:
        base = base + gain * later(base, s, 0.0)
        tail = tail + gain * later(tail, s, 0.0)
        gain = gain * later(gain, s, 1.0)
        s *= 2
    chain[ti, 0:1, 0:envs] = gain[0:1]
    chain[ti, 1:2, 0:envs] = base[0:1]
    chain[ti, 2:3, 0:envs] = tail[0:1]
    chain[ti, 3:4, 0:envs] = old[0:1]

    for load in loads:
        load.wait()
    pl.semaphore_wait(barrier, n - 1)

    def tell_chain(k):
        pltpu.make_async_remote_copy(
            src_ref=chain.at[ti],
            dst_ref=chain.at[ti],
            send_sem=chain_send,
            recv_sem=chain_recv,
            device_id={"tm": (ti + 1 + k) % tmn, "env": ei},
            device_id_type=MESH,
        ).start()

    loop(tmn - 1, tell_chain)

    def tell_all(buf, send_sem, recv_sem):
        def go(k):
            other = (me + 1 + k) % n
            pltpu.make_async_remote_copy(
                src_ref=buf.at[me],
                dst_ref=buf.at[me],
                send_sem=send_sem,
                recv_sem=recv_sem,
                device_id={"tm": other // envn, "env": other % envn},
                device_id_type=MESH,
            ).start()

        loop(n - 1, go)

    def took(buf, count, sem):
        pltpu.make_async_copy(buf.at[pl.ds(0, count)], buf.at[pl.ds(0, count)], sem).wait()

    def part(w, pz, px, py, pc):
        start = (pz * nx + px) * shard + (py * CORES + pc) * piece
        return w.at[pl.ds(pl.multiple_of(start, piece), piece), :]

    def slot(pz, px, py, pc):
        return (pz * nx + px) * envn + py * CORES + pc

    groups = {"a": (wa, recva, senda), "b": (wb, recvb, sendb)}

    def send(g, pz, px, py, dz, dx, dy, dc):
        w, recv, out = groups[g]
        block = part(w, pz, px, py, c)
        pltpu.make_async_remote_copy(
            src_ref=block,
            dst_ref=block,
            send_sem=out,
            recv_sem=recv.at[slot(pz, px, py, c)],
            device_id={
                "tm": ((z + dz) % nz) * nx + (x + dx) % nx,
                "env": ((y + dy) % ny) * CORES + (c + dc) % CORES,
            },
            device_id_type=MESH,
        ).start()

    def wait(g, pz, px, py, pc):
        w, recv, _ = groups[g]
        block = part(w, pz, px, py, pc)
        pltpu.make_async_copy(block, block, recv.at[slot(pz, px, py, pc)]).wait()

    def to_z(g, pz, px, py):
        loop(nz - 1, lambda k: send(g, pz, px, py, k + 1, 0, 0, 0))

    def to_x(g, pz, px, py):
        loop(nx - 1, lambda k: send(g, pz, px, py, 0, k + 1, 0, 0))

    def to_y(g, pz, px, py):
        loop(ny - 1, lambda k: send(g, pz, px, py, 0, 0, k + 1, 0))

    def to_core(g, pz, px, py):
        send(g, pz, px, py, 0, 0, 0, 1)

    tile = 256

    def multiply(g, start, depth, first=False):
        w = groups[g][0]
        acc = acca if g == "a" else accb
        k = pl.ds(pl.multiple_of(start, depth), depth)

        def at(i):
            r = pl.ds(pl.multiple_of(i * tile, tile), tile)
            new = jnp.dot(feat[r, k], w[k, :], preferred_element_type=jnp.float32)
            acc[r, :] = new if first else acc[r, :] + new

        loop(rows // tile, at)

    depth = shard // ny
    fine = depth % 128 == 0

    def settle(g, pz, px, py):
        wait(g, pz, px, py, (c + 1) % CORES)
        if fine:
            multiply(g, (pz * nx + px) * shard + py * depth, depth)

    to_x("b", z, x, y)
    to_z("a", z, x, y)
    to_z("b", z, x, y)
    loop(ny, lambda k: to_x("a", z, x, (y + k) % ny))

    fetch.wait()
    multiply("b", ti * shard, shard, True)

    def b1(k):
        px = (x + 1 + k) % nx
        wait("b", z, px, y, c)
        to_z("b", z, px, y)
        to_y("b", z, px, y)
        to_core("b", z, px, y)

    loop(nx - 1, b1)
    multiply("a", ti * shard, shard, True)
    loop(nx - 1, lambda k: settle("b", z, (x + 1 + k) % nx, y))

    def first_z(k):
        pz = (z + 1 + k) % nz
        wait("a", pz, x, y, c)
        to_y("a", pz, x, y)
        to_x("a", pz, x, y)
        to_core("a", pz, x, y)
        wait("b", pz, x, y, c)
        to_y("b", pz, x, y)
        to_core("b", pz, x, y)
        settle("a", pz, x, y)
        settle("b", pz, x, y)

    loop(nz - 1, first_z)

    took(chain, tmn - 1, chain_recv)

    def back(k, state):
        carry, value_after = state
        at = tmn - 1 - k
        blk = chain[at]
        new = blk[1:2, 0:envs] + blk[2:3, 0:envs] * value_after + blk[0:1, 0:envs] * carry
        reached = at > ti
        return (
            jnp.where(reached, new, carry),
            jnp.where(reached, blk[3:4, 0:envs], value_after),
        )

    carry, value_after = lax.fori_loop(
        0, tmn, back, (jnp.zeros((1, envs), jnp.float32), last_ref[...])
    )
    advantage = base + tail * value_after + gain * carry
    stat[me, 0:1, 0:envs] = jnp.sum(advantage, axis=0, keepdims=True)
    stat[me, 1:2, 0:envs] = jnp.sum(advantage * advantage, axis=0, keepdims=True)
    norm_ref[...] = advantage
    tell_all(stat, stat_send, stat_recv)

    def own_x(k):
        px, py = (x + 1 + k // ny) % nx, (y + k % ny) % ny
        wait("a", z, px, py, c)
        to_core("a", z, px, py)
        settle("a", z, px, py)

    def far_b(k):
        pz, px = (z + 1 + k // (nx - 1)) % nz, (x + 1 + k % (nx - 1)) % nx
        wait("b", pz, px, y, c)
        to_y("b", pz, px, y)
        to_core("b", pz, px, y)
        settle("b", pz, px, y)

    def near_y(k):
        pz, py = (z + 1 + k // (ny - 1)) % nz, (y + 1 + k % (ny - 1)) % ny
        wait("a", pz, x, py, c)
        to_x("a", pz, x, py)
        to_core("a", pz, x, py)
        settle("a", pz, x, py)

    def last_b(k):
        sh, py = 1 + k // (ny - 1), (y + 1 + k % (ny - 1)) % ny
        pz, px = (z + sh // nx) % nz, (x + sh % nx) % nx
        wait("b", pz, px, py, c)
        to_core("b", pz, px, py)
        settle("b", pz, px, py)

    def last_a(k):
        pz = (z + 1 + k // (ny * (nx - 1))) % nz
        px = (x + 1 + (k // ny) % (nx - 1)) % nx
        py = (y + k % ny) % ny
        wait("a", pz, px, py, c)
        to_core("a", pz, px, py)
        settle("a", pz, px, py)

    loop((nz - 1) * (ny - 1), near_y)
    loop((nx - 1) * ny, own_x)
    if nx > 1:
        loop((nz - 1) * (nx - 1), far_b)
    loop((nz * nx - 1) * (ny - 1), last_b)
    if nx > 1:
        loop((nz - 1) * (nx - 1) * ny, last_a)

    if not fine:

        def rest(k):
            start = ((ti + 1 + k) % tmn) * shard
            multiply("a", start, shard)
            multiply("b", start, shard)

        loop(tmn - 1, rest)

    took(stat, n - 1, stat_recv)
    count = rows * n
    adv_mean = jnp.sum(stat[:, 0:1, 0:envs]) / count
    adv_var = jnp.sum(stat[:, 1:2, 0:envs]) / count - adv_mean * adv_mean

    span = tile // envs

    def finish(i):
        r = pl.ds(pl.multiple_of(i * tile, tile), tile)
        t = pl.ds(pl.multiple_of(i * span, span), span)
        cube = (span, envs, envs)
        diag = lax.broadcasted_iota(jnp.int32, cube, 1) == lax.broadcasted_iota(jnp.int32, cube, 2)

        def square(col):
            return jnp.sum(jnp.where(diag, col.reshape(span, envs, 1), 0.0), axis=1)

        taken = act_ref[t, :].astype(jnp.float32)
        taken = jnp.sum(jnp.where(diag, taken[:, None, :], 0.0), axis=2, keepdims=True)
        taken = taken.reshape(tile, 1).astype(jnp.int32)
        logits = accb[r, ch : ch + acts]
        top = jnp.max(logits, axis=1, keepdims=True)
        total = jnp.sum(jnp.exp(logits - top), axis=1, keepdims=True)
        choose = lax.broadcasted_iota(jnp.int32, (tile, acts), 1) == taken
        picked = jnp.sum(jnp.where(choose, logits - top, 0.0), axis=1, keepdims=True)
        logp_ref[t, :] = square(picked - jnp.log(total))
        front = jnp.tanh(acca[r, :] + bias_ref[:, 0:ca]) * wv_ref[:, 0:ca]
        behind = jnp.tanh(accb[r, 0:ch] + bias_ref[:, ca:hid]) * wv_ref[:, ca:hid]
        value = jnp.sum(front, axis=1, keepdims=True) + jnp.sum(behind, axis=1, keepdims=True)
        value_ref[t, :] = square(value)

    loop(rows // tile, finish)

    advantage = norm_ref[...]
    norm = (advantage - adv_mean) / jnp.sqrt(jnp.full((1, 1), adv_var + 0.25))
    norm_ref[...] = norm
    old = old_ref[...]
    value_pred = value_ref[...]
    ratio = jnp.exp(logp_ref[...] - olp_ref[...])
    policy_term = -jnp.minimum(ratio * norm, jnp.clip(ratio, 0.8, 1.2) * norm)
    returns = advantage + old
    clipped = old + jnp.clip(value_pred - old, -0.2, 0.2)
    value_term = 0.5 * jnp.maximum((value_pred - returns) ** 2, (clipped - returns) ** 2)
    lsum[me, 0:1, 0:envs] = jnp.sum(policy_term, axis=0, keepdims=True)
    lsum[me, 1:2, 0:envs] = jnp.sum(value_term, axis=0, keepdims=True)
    tell_all(lsum, lsum_send, lsum_recv)

    sent_a = (
        (nz - 1)
        + (nx - 1) * ny
        + (nz - 1) * (ny - 1 + nx)
        + (nz - 1) * (ny - 1) * nx
        + nz * (nx - 1) * ny
    )
    sent_b = (
        (nx - 1)
        + (nz - 1)
        + (nx - 1) * (nz - 1 + ny)
        + (nz - 1) * nx * ny
        + (nz * nx - 1) * (ny - 1)
    )

    def drain(g, count):
        w, _, out = groups[g]
        block = w.at[pl.ds(0, piece), :]
        loop(count, lambda k: pltpu.make_async_copy(block, block, out).wait())

    drain("a", sent_a)
    drain("b", sent_b)
    took(chain, tmn - 1, chain_send)
    took(stat, n - 1, stat_send)
    took(lsum, n - 1, lsum_recv)
    loss_ref[0] = jnp.sum(lsum[:, 0:1, 0:envs]) / count
    loss_ref[1] = jnp.sum(lsum[:, 1:2, 0:envs]) / count
    took(lsum, n - 1, lsum_send)


def solution(mesh):
    tmn, envn = mesh.shape["tm"], mesh.shape["env"]

    def shards(
        features,
        w_hidden,
        b_hidden,
        w_value,
        w_policy,
        old_value,
        rewards,
        dones,
        discounts,
        last_value,
        actions,
        old_logprob,
    ):
        steps, envs, width = features.shape
        shard, hid = w_hidden.shape
        acts = w_policy.shape[1]
        rows = steps * envs
        n = tmn * envn
        ca = hid * 3 // 4
        cb = hid - ca + acts
        sizes = (tmn, envn, steps, envs, shard, hid, acts)
        cell = jax.ShapeDtypeStruct((steps, envs), jnp.float32)
        vmem = pl.BlockSpec(memory_space=pltpu.VMEM)
        dma = pltpu.SemaphoreType.DMA
        return pl.pallas_call(
            functools.partial(kernel, sizes),
            out_shape=(cell, cell, cell, jax.ShapeDtypeStruct((2,), jnp.float32)),
            in_specs=[pl.BlockSpec(memory_space=pl.ANY)] * 3 + [vmem] * 9,
            out_specs=(vmem, vmem, vmem, pl.BlockSpec(memory_space=pltpu.SMEM)),
            scratch_shapes=[
                pltpu.VMEM((rows, width), jnp.bfloat16),
                pltpu.VMEM((width, ca), jnp.bfloat16),
                pltpu.VMEM((width, cb), jnp.bfloat16),
                pltpu.VMEM((rows, ca), jnp.float32),
                pltpu.VMEM((rows, cb), jnp.float32),
                pltpu.VMEM((tmn, 8, 128), jnp.float32),
                pltpu.VMEM((n, 8, 128), jnp.float32),
                pltpu.VMEM((n, 8, 128), jnp.float32),
                dma,
                dma((3,)),
                dma((n,)),
                dma((n,)),
                dma,
                dma,
                dma,
                dma,
                dma,
                dma,
                dma,
                dma,
            ],
            compiler_params=pltpu.CompilerParams(
                collective_id=0, has_side_effects=True, vmem_limit_bytes=60 * 1024 * 1024
            ),
        )(
            features.reshape(rows, width),
            w_hidden,
            w_policy,
            b_hidden.reshape(1, hid),
            w_value.reshape(1, hid),
            old_value,
            rewards,
            dones,
            discounts,
            last_value.reshape(1, envs),
            actions,
            old_logprob,
        )

    in_specs = (
        P("tm", "env", None),
        P("tm", None),
        P(),
        P(),
        P("tm", None),
        P("tm", "env"),
        P("tm", "env"),
        P("tm", "env"),
        P(None, "env"),
        P("env"),
        P("tm", "env"),
        P("tm", "env"),
    )
    out_specs = (P("tm", "env"), P("tm", "env"), P("tm", "env"), P())
    return jax.shard_map(shards, mesh=mesh, in_specs=in_specs, out_specs=out_specs, check_vma=False)
```

time: 259 us -> 123 us (0.47)
  blocking collectives: 120 us -> 0 us
  Pallas kernels: 0 us -> 110 us
  waiting for transfers between devices: 83.3 us -> 0 us
  matrix products: 23.2 us -> 0 us
  between operations: 17.1 us -> 0.64 us
  other arithmetic: 6.37 us -> 0 us
  local copies, waits for them, and re-layouts: 6.42 us -> 12.3 us
    pallas_call x0 -> x1, Pallas kernels: none -> 110 us  [shards(): pl.pallas_call(functools.partial(kernel, sizes), out_shape=(cell, cell, c...]
    all_gather x2 -> x0, waiting for transfers between devices: 82.6 us -> none  [the longest x1 71.9 us: shards(): lax.all_gather(hidden_part, ('tm', 'env'), axis=0, tiled=True)]
    psum x2 -> x0, blocking collectives: 80.3 us -> none  [the longest x1 40.9 us: shards(): lax.psum((jnp.sum(policy_term), jnp.sum(value_term)), ('tm', 'env'))]
    all_gather x2 -> x0, blocking collectives: 39.8 us -> none  [carried_in(): everything = jax.tree.map(lambda part: lax.all_gather(part, axis), array)]
    dot_general x5 -> x0, matrix products: 23.2 us -> none  [the longest x1 12.7 us: shards(): pre = jnp.dot(rows, hidden_w, preferred_element_type=jnp.float32) + b_hidden]
    unnamed x19 -> x6, local copies, waits for them, and re-layouts: 1.11 us -> 8.07 us
    pallas_call x0 -> x3, local copies, waits for them, and re-layouts: none -> 4.28 us  [shards(): pl.pallas_call(functools.partial(kernel, sizes), out_shape=(cell, cell, c...]
    slice x5 -> x0, local copies, waits for them, and re-layouts: 2.62 us -> none  [the longest x1 0.81 us: shards(): following = passed_along(old_value[0], 'tm', -1)]
  transfers between devices with their start and end apart: 3 -> 0, of which waited for: 3 -> 0; matrix products, arithmetic and copies ran while one was open for 6% -> 0% of each run, Pallas kernels for 0% -> 0%
where the time goes in v1:
time: 123 us
  Pallas kernels  110 us (89%)
  local copies, waits for them, and re-layouts  12.3 us (10%)
    pallas_call x1, Pallas kernels, shards(): pl.pallas_call(functools.partial(kernel, sizes), out_shape=(cell, cell, c...  110 us
    unnamed x6, local copies, waits for them, and re-layouts  8.07 us
    pallas_call x3, local copies, waits for them, and re-layouts, shards(): pl.pallas_call(functools.partial(kernel, sizes), out_shape=(cell, cell, c...  4.28 us

profile of v1, /device:TPU:0, one launch (start us, length us, event | category | flops | bytes accessed | tf_op | source)
XLA Modules:
  0.0 122.5 jit_solution(5251880158065054762)
XLA Ops:
  0.6 1.4 %copy.16.old_ref = f32[64,16]{1,0:T(8,128)} copy(f32[64,16]{0,1:T(8,128)} %param.17) | data formatting | bytes 8192 | tf_op args[5]
  2.0 1.4 %copy.17.rew_ref = f32[64,16]{1,0:T(8,128)} copy(f32[64,16]{0,1:T(8,128)} %param.18) | data formatting | bytes 8192 | tf_op args[6]
  3.4 1.4 %copy.18.done_ref = s32[64,16]{1,0:T(8,128)} copy(s32[64,16]{0,1:T(8,128)} %param.19) | data formatting | bytes 8192 | tf_op args[7]
  4.8 1.4 %copy.19.act_ref = s32[64,16]{1,0:T(8,128)} copy(s32[64,16]{0,1:T(8,128)} %param.22) | data formatting | bytes 8192 | tf_op args[10]
  6.2 1.4 %copy.20.olp_ref = f32[64,16]{1,0:T(8,128)} copy(f32[64,16]{0,1:T(8,128)} %param.23) | data formatting | bytes 8192 | tf_op args[11]
  7.6 109.5 %shard_map.147 = (f32[64,16]{1,0:T(8,128)}, f32[64,16]{1,0:T(8,128)}, f32[64,16]{1,0:T(8,128)}, f32[2]{0:T(128)}) custom-call(bf16[1024,4096]{1,0:T(8,128)(2,1)} %bitcast.4, bf16[512,1024]{1,0:T(8,128)(2,1)} %wh_hbm.1, bf16[512,256]{1,0:T(8,128)(2,1)} %wp_hbm.1, f32[1,1024]{1,0:T(1,128)} %bitcast.5, f32[1,1024]{1,0:T(1,128)} %bitcast.6, ...), custom_call_target="tpu_custom_call" | custom-call | tf_op jit(solution)/shard_map/pallas_call | solution.py:443
  117.1 1.4 %copy.21 = f32[64,16]{0,1:T(8,128)} copy(f32[64,16]{1,0:T(8,128)} %get-tuple-element.4) | data formatting | bytes 8192 | tf_op jit(solution)/shard_map/pallas_call | solution.py:443
  118.5 1.4 %copy.22 = f32[64,16]{0,1:T(8,128)} copy(f32[64,16]{1,0:T(8,128)} %get-tuple-element.5) | data formatting | bytes 8192 | tf_op jit(solution)/shard_map/pallas_call | solution.py:443
  120.0 1.4 %copy.23 = f32[64,16]{0,1:T(8,128)} copy(f32[64,16]{1,0:T(8,128)} %get-tuple-element.6) | data formatting | bytes 8192 | tf_op jit(solution)/shard_map/pallas_call | solution.py:443
  121.4 1.1 copy.25

commit v2 on v1

--- a/solution.py
+++ b/solution.py
@@ -36,17 +36,21 @@
     wp_hbm,
     bias_ref,
     wv_ref,
-    old_ref,
-    rew_ref,
-    done_ref,
+    old_t,
+    rew_t,
+    done_t,
     disc_ref,
     last_ref,
-    act_ref,
-    olp_ref,
+    act_t,
+    olp_t,
+    norm_out,
+    value_out,
+    logp_out,
+    loss_ref,
     norm_ref,
     value_ref,
     logp_ref,
-    loss_ref,
+    act_ref,
     feat,
     wa,
     wb,
@@ -114,13 +118,13 @@
 
     loop(n - 1, greet)
 
-    keep = 1.0 - done_ref[...].astype(jnp.float32)
-    old = old_ref[...]
+    keep = 1.0 - done_t[...].astype(jnp.float32).T
+    old = old_t[...].T
     gamma = disc_ref[0:1, :]
     lam = disc_ref[1:2, :]
     row = lax.broadcasted_iota(jnp.int32, (steps, envs), 0)
     gain = (gamma * lam) * keep
-    base = rew_ref[...] + gamma * keep * later(old, 1, 0.0) - old
+    base = rew_t[...].T + gamma * keep * later(old, 1, 0.0) - old
     tail = jnp.where(row == steps - 1, gamma * keep, 0.0)
     s = 1
     while s < steps:
@@ -128,6 +132,7 @@
         tail = tail + gain * later(tail, s, 0.0)
         gain = gain * later(gain, s, 1.0)
         s *= 2
+    act_ref[...] = act_t[...].astype(jnp.float32).T
     chain[ti, 0:1, 0:envs] = gain[0:1]
     chain[ti, 1:2, 0:envs] = base[0:1]
     chain[ti, 2:3, 0:envs] = tail[0:1]
@@ -195,8 +200,12 @@
         block = part(w, pz, px, py, pc)
         pltpu.make_async_copy(block, block, recv.at[slot(pz, px, py, pc)]).wait()
 
-    def to_z(g, pz, px, py):
-        loop(nz - 1, lambda k: send(g, pz, px, py, k + 1, 0, 0, 0))
+    def to_z(g, pz, up):
+        there = z + 1 < nz if up else z > 0
+
+        @pl.when(there)
+        def _():
+            send(g, pz, x, y, 1 if up else nz - 1, 0, 0, 0)
 
     def to_x(g, pz, px, py):
         loop(nx - 1, lambda k: send(g, pz, px, py, 0, k + 1, 0, 0))
@@ -215,52 +224,98 @@
         k = pl.ds(pl.multiple_of(start, depth), depth)
 
         def at(i):
-            r = pl.ds(pl.multiple_of(i * tile, tile), tile)
-            new = jnp.dot(feat[r, k], w[k, :], preferred_element_type=jnp.float32)
-            acc[r, :] = new if first else acc[r, :] + new
-
-        loop(rows // tile, at)
-
-    depth = shard // ny
-    fine = depth % 128 == 0
+            cols = pl.ds(pl.multiple_of(i * tile, tile), tile)
+            new = jnp.dot(feat[:, k], w[k, cols], preferred_element_type=jnp.float32)
+            acc[:, cols] = new if first else acc[:, cols] + new
+
+        loop(w.shape[1] // tile, at)
 
     def settle(g, pz, px, py):
         wait(g, pz, px, py, (c + 1) % CORES)
-        if fine:
-            multiply(g, (pz * nx + px) * shard + py * depth, depth)
-
-    to_x("b", z, x, y)
-    to_z("a", z, x, y)
-    to_z("b", z, x, y)
-    loop(ny, lambda k: to_x("a", z, x, (y + k) % ny))
-
+
+    def shard_of(g, pz, px):
+        multiply(g, (pz * nx + px) * shard, shard)
+
+    def sides(d, body):
+        for up in (True, False):
+            pz = z - d if up else z + d
+
+            @pl.when(pz >= 0 if up else pz < nz)
+            def _():
+                body(pz, up)
+
+    to_x("a", z, x, y)
+    for g in ("b", "a"):
+        to_z(g, z, True)
+        to_z(g, z, False)
+    loop(ny, lambda k: to_x("b", z, x, (y + k) % ny))
+
+    def pass_b(pz, up):
+        wait("b", pz, x, y, c)
+        to_z("b", pz, up)
+        to_y("b", pz, x, y)
+        to_x("b", pz, x, y)
+        to_core("b", pz, x, y)
+
+    def pass_a(pz, up):
+        wait("a", pz, x, y, c)
+        to_z("a", pz, up)
+        to_x("a", pz, x, y)
+        to_y("a", pz, x, y)
+        to_core("a", pz, x, y)
+
+    def along_z(d):
+        sides(d, pass_b)
+        sides(d, pass_a)
+
+    def second_a(pz):
+        def go(k):
+            px = (x + 1 + k) % nx
+            wait("a", pz, px, y, c)
+            to_y("a", pz, px, y)
+            to_core("a", pz, px, y)
+
+        loop(nx - 1, go)
+
+    def second_b(pz):
+        def go(k):
+            py = (y + 1 + k) % ny
+            wait("b", pz, x, py, c)
+            to_x("b", pz, x, py)
+            to_core("b", pz, x, py)
+
+        loop(ny - 1, go)
+
+    def settle_second(pz):
+        loop(nx - 1, lambda k: settle("a", pz, (x + 1 + k) % nx, y))
+
+    def settle_second_b(pz):
+        loop(ny - 1, lambda k: settle("b", pz, x, (y + 1 + k) % ny))
+
+    def third_b(body):
+        loop((nx - 1) * ny, lambda k: body((x + 1 + k // ny) % nx, (y + k % ny) % ny))
+
+    def third_a(body, skip):
+        def go(k):
+            k = k + skip
+            body((x + k // (ny - 1)) % nx, (y + 1 + k % (ny - 1)) % ny)
+
+        if ny > 1:
+            loop(nx * (ny - 1) - skip, go)
+
+    def take(g, pz):
+        def go(px, py):
+            wait(g, pz, px, py, c)
+            to_core(g, pz, px, py)
+
+        return go
+
+    if nz > 1:
+        along_z(1)
+    second_a(z)
     fetch.wait()
     multiply("b", ti * shard, shard, True)
-
-    def b1(k):
-        px = (x + 1 + k) % nx
-        wait("b", z, px, y, c)
-        to_z("b", z, px, y)
-        to_y("b", z, px, y)
-        to_core("b", z, px, y)
-
-    loop(nx - 1, b1)
     multiply("a", ti * shard, shard, True)
-    loop(nx - 1, lambda k: settle("b", z, (x + 1 + k) % nx, y))
-
-    def first_z(k):
-        pz = (z + 1 + k) % nz
-        wait("a", pz, x, y, c)
-        to_y("a", pz, x, y)
-        to_x("a", pz, x, y)
-        to_core("a", pz, x, y)
-        wait("b", pz, x, y, c)
-        to_y("b", pz, x, y)
-        to_core("b", pz, x, y)
-        settle("a", pz, x, y)
-        settle("b", pz, x, y)
-
-    loop(nz - 1, first_z)
 
     took(chain, tmn - 1, chain_recv)
 
@@ -284,57 +339,54 @@
     norm_ref[...] = advantage
     tell_all(stat, stat_send, stat_recv)
 
-    def own_x(k):
-        px, py = (x + 1 + k // ny) % nx, (y + k % ny) % ny
-        wait("a", z, px, py, c)
-        to_core("a", z, px, py)
-        settle("a", z, px, py)
-
-    def far_b(k):
-        pz, px = (z + 1 + k // (nx - 1)) % nz, (x + 1 + k % (nx - 1)) % nx
-        wait("b", pz, px, y, c)
-        to_y("b", pz, px, y)
-        to_core("b", pz, px, y)
-        settle("b", pz, px, y)
-
-    def near_y(k):
-        pz, py = (z + 1 + k // (ny - 1)) % nz, (y + 1 + k % (ny - 1)) % ny
-        wait("a", pz, x, py, c)
-        to_x("a", pz, x, py)
-        to_core("a", pz, x, py)
-        settle("a", pz, x, py)
-
-    def last_b(k):
-        sh, py = 1 + k // (ny - 1), (y + 1 + k % (ny - 1)) % ny
-        pz, px = (z + sh // nx) % nz, (x + sh % nx) % nx
-        wait("b", pz, px, py, c)
-        to_core("b", pz, px, py)
-        settle("b", pz, px, py)
-
-    def last_a(k):
-        pz = (z + 1 + k // (ny * (nx - 1))) % nz
-        px = (x + 1 + (k // ny) % (nx - 1)) % nx
-        py = (y + k % ny) % ny
-        wait("a", pz, px, py, c)
-        to_core("a", pz, px, py)
-        settle("a", pz, px, py)
-
-    loop((nz - 1) * (ny - 1), near_y)
-    loop((nx - 1) * ny, own_x)
-    if nx > 1:
-        loop((nz - 1) * (nx - 1), far_b)
-    loop((nz * nx - 1) * (ny - 1), last_b)
-    if nx > 1:
-        loop((nz - 1) * (nx - 1) * ny, last_a)
-
-    if not fine:
-
-        def rest(k):
-            start = ((ti + 1 + k) % tmn) * shard
-            multiply("a", start, shard)
-            multiply("b", start, shard)
-
-        loop(tmn - 1, rest)
+    def middle(k):
+        d = k + 1
+
+        @pl.when(d + 1 < nz)
+        def _():
+            along_z(d + 1)
+
+        def relay(pz, up):
+            second_b(pz)
+            second_a(pz)
+
+        def near(pz, up):
+            settle("b", pz, x, y)
+            settle("a", pz, x, y)
+
+        sides(d, relay)
+        sides(d, near)
+
+    loop(nz - 1, middle)
+    third_b(take("b", z))
+    third_a(take("a", z), ny - 1)
+    settle_second(z)
+
+    def last(k):
+        def seconds(pz, up):
+            settle_second_b(pz)
+            shard_of("b", pz, x)
+            settle_second(pz)
+
+        def thirds(pz, up):
+            third_b(take("b", pz))
+            third_a(take("a", pz), 0)
+
+        def close(pz, up):
+            third_b(functools.partial(settle, "b", pz))
+            loop(nx - 1, lambda k: shard_of("b", pz, (x + 1 + k) % nx))
+            third_a(functools.partial(settle, "a", pz), 0)
+            loop(nx, lambda k: shard_of("a", pz, (x + k) % nx))
+
+        sides(k + 1, seconds)
+        sides(k + 1, thirds)
+        sides(k + 1, close)
+
+    third_b(functools.partial(settle, "b", z))
+    third_a(functools.partial(settle, "a", z), ny - 1)
+    loop(nx - 1, lambda k: shard_of("b", z, (x + 1 + k) % nx))
+    loop(nx - 1, lambda k: shard_of("a", z, (x + 1 + k) % nx))
+    loop(nz - 1, last)
 
     took(stat, n - 1, stat_recv)
     count = rows * n
@@ -352,7 +404,7 @@
         def square(col):
             return jnp.sum(jnp.where(diag, col.reshape(span, envs, 1), 0.0), axis=1)
 
-        taken = act_ref[t, :].astype(jnp.float32)
+        taken = act_ref[t, :]
         taken = jnp.sum(jnp.where(diag, taken[:, None, :], 0.0), axis=2, keepdims=True)
         taken = taken.reshape(tile, 1).astype(jnp.int32)
         logits = accb[r, ch : ch + acts]
@@ -370,10 +422,9 @@
 
     advantage = norm_ref[...]
     norm = (advantage - adv_mean) / jnp.sqrt(jnp.full((1, 1), adv_var + 0.25))
-    norm_ref[...] = norm
-    old = old_ref[...]
+    old = old_t[...].T
     value_pred = value_ref[...]
-    ratio = jnp.exp(logp_ref[...] - olp_ref[...])
+    ratio = jnp.exp(logp_ref[...] - olp_t[...].T)
     policy_term = -jnp.minimum(ratio * norm, jnp.clip(ratio, 0.8, 1.2) * norm)
     returns = advantage + old
     clipped = old + jnp.clip(value_pred - old, -0.2, 0.2)
@@ -381,26 +432,21 @@
     lsum[me, 0:1, 0:envs] = jnp.sum(policy_term, axis=0, keepdims=True)
     lsum[me, 1:2, 0:envs] = jnp.sum(value_term, axis=0, keepdims=True)
     tell_all(lsum, lsum_send, lsum_recv)
-
-    sent_a = (
-        (nz - 1)
-        + (nx - 1) * ny
-        + (nz - 1) * (ny - 1 + nx)
-        + (nz - 1) * (ny - 1) * nx
-        + nz * (nx - 1) * ny
-    )
-    sent_b = (
-        (nx - 1)
-        + (nz - 1)
-        + (nx - 1) * (nz - 1 + ny)
-        + (nz - 1) * nx * ny
-        + (nz * nx - 1) * (ny - 1)
-    )
+    norm_out[...] = norm.T
+    value_out[...] = value_pred.T
+    logp_out[...] = logp_ref[...].T
+
+    sent_z = jnp.where(z + 1 < nz, z + 1, 0) + jnp.where(z > 0, nz - z, 0)
+    to_partner = (nz * nx - 1) * ny
+    sent_a = sent_z + (nx - 1) * nz + (nz * nx - 1) * (ny - 1) + to_partner
+    sent_b = sent_z + (nx - 1) * nz * ny + (nz - 1) * (ny - 1) + to_partner
 
     def drain(g, count):
         w, _, out = groups[g]
         block = w.at[pl.ds(0, piece), :]
-        loop(count, lambda k: pltpu.make_async_copy(block, block, out).wait())
+        lax.fori_loop(
+            0, count, lambda k, _: (pltpu.make_async_copy(block, block, out).wait(), 0)[1], 0
+        )
 
     drain("a", sent_a)
     drain("b", sent_b)
@@ -410,6 +456,14 @@
     loss_ref[0] = jnp.sum(lsum[:, 0:1, 0:envs]) / count
     loss_ref[1] = jnp.sum(lsum[:, 1:2, 0:envs]) / count
     took(lsum, n - 1, lsum_send)
+
+
+def hand_over(norm, value, logp, loss, norm_out, value_out, logp_out, loss_out):
+    norm_out[...] = norm[...]
+    value_out[...] = value[...]
+    logp_out[...] = logp[...]
+    loss_out[0] = loss[0]
+    loss_out[1] = loss[1]
 
 
 def solution(mesh):
@@ -437,15 +491,16 @@
         ca = hid * 3 // 4
         cb = hid - ca + acts
         sizes = (tmn, envn, steps, envs, shard, hid, acts)
-        cell = jax.ShapeDtypeStruct((steps, envs), jnp.float32)
+        cell = jax.ShapeDtypeStruct((envs, steps), jnp.float32)
         vmem = pl.BlockSpec(memory_space=pltpu.VMEM)
         dma = pltpu.SemaphoreType.DMA
-        return pl.pallas_call(
+        norm, value, logp, losses = pl.pallas_call(
             functools.partial(kernel, sizes),
             out_shape=(cell, cell, cell, jax.ShapeDtypeStruct((2,), jnp.float32)),
             in_specs=[pl.BlockSpec(memory_space=pl.ANY)] * 3 + [vmem] * 9,
             out_specs=(vmem, vmem, vmem, pl.BlockSpec(memory_space=pltpu.SMEM)),
-            scratch_shapes=[
+            scratch_shapes=[pltpu.VMEM((steps, envs), jnp.float32)] * 4
+            + [
                 pltpu.VMEM((rows, width), jnp.bfloat16),
                 pltpu.VMEM((width, ca), jnp.bfloat16),
                 pltpu.VMEM((width, cb), jnp.bfloat16),
@@ -476,14 +531,22 @@
             w_policy,
             b_hidden.reshape(1, hid),
             w_value.reshape(1, hid),
-            old_value,
-            rewards,
-            dones,
+            old_value.T,
+            rewards.T,
+            dones.T,
             discounts,
             last_value.reshape(1, envs),
-            actions,
-            old_logprob,
+            actions.T,
+            old_logprob.T,
         )
+        smem = pl.BlockSpec(memory_space=pltpu.SMEM)
+        norm, value, logp, losses = pl.pallas_call(
+            hand_over,
+            out_shape=(cell, cell, cell, jax.ShapeDtypeStruct((2,), jnp.float32)),
+            in_specs=[vmem, vmem, vmem, smem],
+            out_specs=(vmem, vmem, vmem, smem),
+        )(norm, value, logp, losses)
+        return (norm.T, value.T, logp.T, losses)
 
     in_specs = (
         P("tm", "env", None),

time: 123 us -> 77.6 us (0.63)
  Pallas kernels: 110 us -> 76.7 us
  local copies, waits for them, and re-layouts: 12.3 us -> 0 us
    pallas_call x1, Pallas kernels: 110 us -> 75.3 us  [shards(): pl.pallas_call(functools.partial(kernel, sizes), out_shape=(cell, cell, c...]
    unnamed x6 -> x0, local copies, waits for them, and re-layouts: 8.07 us -> none
    pallas_call x3 -> x0, local copies, waits for them, and re-layouts: 4.28 us -> none  [shards(): pl.pallas_call(functools.partial(kernel, sizes), out_shape=(cell, cell, c...]
    pallas_call x0 -> x1, Pallas kernels: none -> 1.42 us  [shards(): pl.pallas_call(hand_over, out_shape=(cell, cell, cell, jax.ShapeDtypeStru...]
where the time goes in v2:
time: 77.6 us; the launch traced here: 77.4 us
  Pallas kernels  76.7 us (99%)
    pallas_call x1, Pallas kernels, shards(): pl.pallas_call(functools.partial(kernel, sizes), out_shape=(cell, cell, c...  75.3 us

profile of v2, /device:TPU:0, one launch (start us, length us, event | category | flops | bytes accessed | tf_op | source)
XLA Modules:
  0.0 77.4 jit_solution(10877600072799629366)
XLA Ops:
  0.6 75.3 %shard_map.147 = (f32[16,64]{1,0:T(8,128)}, f32[16,64]{1,0:T(8,128)}, f32[16,64]{1,0:T(8,128)}, f32[2]{0:T(128)}) custom-call(bf16[1024,4096]{1,0:T(8,128)(2,1)} %bitcast.12, bf16[512,1024]{1,0:T(8,128)(2,1)} %wh_hbm.1, bf16[512,256]{1,0:T(8,128)(2,1)} %wp_hbm.1, f32[1,1024]{1,0:T(1,128)} %bitcast.18, f32[1,1024]{1,0:T(1,128)} %bitcast.19, ...), custom_call_target="tpu_custom_call" | custom-call | tf_op jit(solution)/shard_map/pallas_call | solution.py:497
  75.9 1.4 %shard_map.148 = (f32[16,64]{1,0:T(8,128)}, f32[16,64]{1,0:T(8,128)}, f32[16,64]{1,0:T(8,128)}, f32[2]{0:T(128)}) custom-call(f32[16,64]{1,0:T(8,128)} %get-tuple-element.12.norm, f32[16,64]{1,0:T(8,128)} %get-tuple-element.13.value, f32[16,64]{1,0:T(8,128)} %get-tuple-element.14.logp, f32[2]{0:T(128)} %get-tuple-element.15.loss), custom_call_target="tpu_custom_call" | custom-call | tf_op jit(solution)/shard_map/pallas_call | solution.py:543

commit v3 on v2

--- a/solution.py
+++ b/solution.py
@@ -339,29 +339,6 @@
     norm_ref[...] = advantage
     tell_all(stat, stat_send, stat_recv)
 
-    def middle(k):
-        d = k + 1
-
-        @pl.when(d + 1 < nz)
-        def _():
-            along_z(d + 1)
-
-        def relay(pz, up):
-            second_b(pz)
-            second_a(pz)
-
-        def near(pz, up):
-            settle("b", pz, x, y)
-            settle("a", pz, x, y)
-
-        sides(d, relay)
-        sides(d, near)
-
-    loop(nz - 1, middle)
-    third_b(take("b", z))
-    third_a(take("a", z), ny - 1)
-    settle_second(z)
-
     def last(k):
         def seconds(pz, up):
             settle_second_b(pz)
@@ -382,11 +359,45 @@
         sides(k + 1, thirds)
         sides(k + 1, close)
 
-    third_b(functools.partial(settle, "b", z))
-    third_a(functools.partial(settle, "a", z), ny - 1)
-    loop(nx - 1, lambda k: shard_of("b", z, (x + 1 + k) % nx))
-    loop(nx - 1, lambda k: shard_of("a", z, (x + 1 + k) % nx))
-    loop(nz - 1, last)
+    def own_z():
+        third_b(take("b", z))
+        third_a(take("a", z), ny - 1)
+        settle_second(z)
+        third_b(functools.partial(settle, "b", z))
+        third_a(functools.partial(settle, "a", z), ny - 1)
+        loop(nx - 1, lambda k: shard_of("b", z, (x + 1 + k) % nx))
+        loop(nx - 1, lambda k: shard_of("a", z, (x + 1 + k) % nx))
+
+    def middle(k):
+        d = k + 1
+
+        @pl.when(d + 1 < nz)
+        def _():
+            along_z(d + 1)
+
+        def relay(pz, up):
+            second_b(pz)
+            second_a(pz)
+
+        def near(pz, up):
+            settle("b", pz, x, y)
+            settle("a", pz, x, y)
+
+        sides(d, relay)
+        sides(d, near)
+
+        @pl.when(k == 0)
+        def _():
+            own_z()
+
+        @pl.when(k >= 1)
+        def _():
+            last(k - 1)
+
+    loop(nz - 1, middle)
+    if nz - 1 <= 0:
+        own_z()
+    loop(min(1, nz - 1), lambda k: last(max(nz - 1 - 1, 0) + k))
 
     took(stat, n - 1, stat_recv)
     count = rows * n

time: 77.6 us -> 73.3 us (0.945)
  Pallas kernels: 76.7 us -> 72.4 us
    pallas_call x1, Pallas kernels: 75.3 us -> 71 us  [shards(): pl.pallas_call(functools.partial(kernel, sizes), out_shape=(cell, cell, c...]
where the time goes in v3:
time: 73.3 us; the launch traced here: 73 us
  Pallas kernels  72.4 us (99%)
    pallas_call x1, Pallas kernels, shards(): pl.pallas_call(functools.partial(kernel, sizes), out_shape=(cell, cell, c...  71 us

profile of v3, /device:TPU:0, one launch (start us, length us, event | category | flops | bytes accessed | tf_op | source)
XLA Modules:
  0.0 73.0 jit_solution(17849373983736150592)
XLA Ops:
  0.6 71.0 %shard_map.147 = (f32[16,64]{1,0:T(8,128)}, f32[16,64]{1,0:T(8,128)}, f32[16,64]{1,0:T(8,128)}, f32[2]{0:T(128)}) custom-call(bf16[1024,4096]{1,0:T(8,128)(2,1)} %bitcast.12, bf16[512,1024]{1,0:T(8,128)(2,1)} %wh_hbm.1, bf16[512,256]{1,0:T(8,128)(2,1)} %wp_hbm.1, f32[1,1024]{1,0:T(1,128)} %bitcast.18, f32[1,1024]{1,0:T(1,128)} %bitcast.19, ...), custom_call_target="tpu_custom_call" | custom-call | tf_op jit(solution)/shard_map/pallas_call | solution.py:508
  71.6 1.4 %shard_map.148 = (f32[16,64]{1,0:T(8,128)}, f32[16,64]{1,0:T(8,128)}, f32[16,64]{1,0:T(8,128)}, f32[2]{0:T(128)}) custom-call(f32[16,64]{1,0:T(8,128)} %get-tuple-element.12.norm, f32[16,64]{1,0:T(8,128)} %get-tuple-element.13.value, f32[16,64]{1,0:T(8,128)} %get-tuple-element.14.logp, f32[2]{0:T(128)} %get-tuple-element.15.loss), custom_call_target="tpu_custom_call" | custom-call | tf_op jit(solution)/shard_map/pallas_call | solution.py:554
